TPU v7x, 512 devices: a whole 4x8x8 slice. The times are simulated.
512 devices in a mesh: seq: 32 (over x_hi, y, core), doc: 16 (over x_lo, z).
Axes of the slice: x: 4 (x_hi: 2, x_lo: 2; x = x_hi * 2 + x_lo), y: 8, z: 8, core: 2. Of those that a mesh axis runs over, the one named last changes fastest.
Arguments:
- hidden: bfloat16 [16, 4096, 768], P('doc', 'seq'), may hold values from -3 to 3
- queries: bfloat16 [16, 4096, 768], P('doc', 'seq'), may hold values from -8 to 8
- key_states: bfloat16 [16, 4096, 768], P('doc', 'seq'), may hold values from -8 to 8
- values: bfloat16 [16, 4096, 768], P('doc', 'seq'), may hold values from -8 to 8
- targets: int32 [16, 4096], P('doc', 'seq'), may hold values from 0 to 26623
- lengths: int32 [16], replicated, may hold values from 2048 to 4096
- keep_rank: int32 [1], replicated, may hold values from 0 to 99
- out_weight: bfloat16 [768, 768], replicated, may hold values from -0.21875 to 0.21875
- final_gain: float32 [768], replicated, may hold values from 0.5 to 1.5
- unembed: bfloat16 [768, 26624], P(None, 'doc'), may hold values from -0.390625 to 0.390625
Outputs:
- token_nll: float32 [16, 4096], P('doc', 'seq')
- log_perplexity: float32 [16], replicated
- acceptance: float32 [16], replicated
All inputs are finite; a program needn't handle non-finite values.
Results may differ from a plain program's by a relative error of at most 0.007.
Values may be sent and summed in bfloat16 or wider, within the bound.
A program may use at most 64 MiB of HBM per device.

v0:
```python
import math
import jax
import jax.numpy as jnp
from jax import lax
from jax.sharding import Mesh
from jax.sharding import PartitionSpec as P

HEADS = 12
HEAD_DIM = 64
ROT = 16
DOC = ("doc_0", "doc_1")
NEGATIVE = -1e30
ROTARY_BASE = 10000.0
NORM_EPSILON = 1e-05
SPREAD_EPSILON = 0.0001


def in_order(blocks, dim):
    blocks = jnp.moveaxis(blocks, 0, dim)
    shape = blocks.shape
    return blocks.reshape(*shape[:dim], shape[dim] * shape[dim + 1], *shape[dim + 2 :])


def all_blocks(array, axes, turns):
    blocks = array[None]
    for k in turns:
        blocks = lax.all_gather(blocks, axes[k], axis=0, tiled=True)
    held = [lax.axis_size(axes[k]) for k in reversed(turns)]
    blocks = blocks.reshape(*held, *array.shape)
    turned = sorted(range(len(turns)), key=lambda place: turns[len(turns) - 1 - place])
    return blocks.transpose(*turned, *range(len(turns), blocks.ndim)).reshape(-1, *array.shape)


def gathered_by_axis(array, axes, turns, dim):
    return in_order(all_blocks(array, axes, turns), dim)


def from_everyone(array, axis):
    copies = jnp.broadcast_to(array, (lax.axis_size(axis), *array.shape))
    return lax.all_to_all(copies, axis, split_axis=0, concat_axis=0, tiled=True)


def collected_together(array, axis):
    leaves = jax.tree.leaves(array)
    turns = sorted(range(len(leaves)), key=lambda k: -leaves[k].size)
    width = (1, *leaves[turns[0]].shape)[-1]
    lines = [
        jnp.pad(leaves[k].reshape(-1), (0, -leaves[k].size % width)).reshape(-1, width)
        for k in turns
    ]
    both, at, found = (from_everyone(jnp.concatenate(lines), axis), 0, {})
    for k, line in zip(turns, lines):
        piece = both[:, at : at + len(line)].reshape(len(both), -1)
        found[k] = piece[:, : leaves[k].size].reshape(-1, *leaves[k].shape)
        at += len(line)
    numbers = iter(range(len(leaves)))
    return jax.tree.map(lambda _: found[next(numbers)], array)


def folded_in_pairs(pieces, combine):
    while len(jax.tree.leaves(pieces)[0]) > 1:
        pieces = jax.vmap(combine)(
            *(jax.tree.map(lambda part: part[side::2], pieces) for side in (0, 1))
        )
    return jax.tree.map(lambda part: part[0], pieces)


def joined_all(array, axis, combine):
    pieces = collected_together(array, axis)
    return folded_in_pairs(pieces, combine)


def over_copies(array, axis):
    everything = from_everyone(array, axis)
    return jnp.sum(everything, axis=0)


def rotate(block, first_row):
    row_count = block.shape[0]
    half_rot = ROT // 2
    where_at = (first_row + jnp.arange(row_count, dtype=jnp.int32)).astype(jnp.float32)
    inv_freq = ROTARY_BASE ** (
        -2.0 * jnp.arange(half_rot, dtype=jnp.int32).astype(jnp.float32) / ROT
    )
    angles = where_at[:, None] * inv_freq[None, :]
    cosine = jnp.cos(angles)[:, None, :]
    sine_part = jnp.sin(angles)[:, None, :]
    per_head = block.reshape(row_count, HEADS, HEAD_DIM)
    low_half = per_head[:, :, :half_rot]
    high_half = per_head[:, :, half_rot:ROT]
    turned = jnp.concatenate(
        [
            low_half * cosine - high_half * sine_part,
            high_half * cosine + low_half * sine_part,
            per_head[:, :, ROT:],
        ],
        axis=2,
    )
    return turned.reshape(row_count, HEADS * HEAD_DIM)


def combine(first_part, second_part):
    top_first, total_first, pick_first = first_part
    top_second, total_second, pick_second = second_part
    top_score = jnp.maximum(top_first, top_second)
    merged = total_first * jnp.exp(top_first - top_score) + total_second * jnp.exp(
        top_second - top_score
    )
    return (top_score, merged, pick_first + pick_second)


def accept(log_perplexity, keep_rank):
    doc_count = log_perplexity.shape[0]
    center = log_perplexity - jnp.mean(log_perplexity)
    spread = jnp.sqrt(jnp.mean(center * center) + SPREAD_EPSILON)
    ordered = jnp.sort(log_perplexity)
    scaled_rank = keep_rank[0] * (doc_count - 1)
    low_index = scaled_rank // 99
    high_index = jnp.minimum(low_index + 1, doc_count - 1)
    fraction = (scaled_rank - 99 * low_index).astype(jnp.float32) / 99.0
    places = jnp.arange(doc_count, dtype=jnp.int32)
    low_value = jnp.sum(jnp.where(places == low_index, ordered, 0.0))
    high_value = jnp.sum(jnp.where(places == high_index, ordered, 0.0))
    rank_level = (1.0 - fraction) * low_value + fraction * high_value
    return jax.nn.sigmoid((rank_level - log_perplexity) / spread)


def shards(
    hidden,
    queries,
    key_states,
    values,
    targets,
    lengths,
    keep_rank,
    out_weight,
    final_gain,
    unembed,
):
    tok_rows = queries.shape[1]
    seq_index = lax.axis_index("seq")
    first_row = seq_index * tok_rows
    turned_q = rotate(queries[0].astype(jnp.float32), first_row).astype(jnp.bfloat16)
    turned_k = rotate(key_states[0].astype(jnp.float32), first_row).astype(jnp.bfloat16)
    query_heads = turned_q.reshape(tok_rows, HEADS, HEAD_DIM)
    query_place = first_row + jnp.arange(tok_rows, dtype=jnp.int32)
    last_row = first_row + tok_rows - 1
    score_scale = 1.0 / math.sqrt(HEAD_DIM)
    key_value = jnp.stack([turned_k, values[0]])
    start_state = (
        jnp.full((HEADS, tok_rows), NEGATIVE, jnp.float32),
        jnp.zeros((HEADS, tok_rows), jnp.float32),
        jnp.zeros((HEADS, tok_rows, HEAD_DIM), jnp.float32),
    )

    def absorb(running, pair_block, begin_at):
        row_count = pair_block.shape[1]
        key_heads = pair_block[0].reshape(row_count, HEADS, HEAD_DIM)
        value_heads = pair_block[1].reshape(row_count, HEADS, HEAD_DIM)
        scores = (
            jnp.einsum("qhd,khd->hqk", query_heads, key_heads, preferred_element_type=jnp.float32)
            * score_scale
        )
        key_place = begin_at + jnp.arange(row_count, dtype=jnp.int32)
        allowed = key_place[None, None, :] <= query_place[None, :, None]
        scores = jnp.where(allowed, scores, NEGATIVE)
        old_top, totals, summed = running
        top_score = jnp.maximum(old_top, jnp.max(scores, axis=2))
        weights = jnp.where(allowed, jnp.exp(scores - top_score[:, :, None]), 0.0)
        factor = jnp.exp(old_top - top_score)
        totals = totals * factor + jnp.sum(weights, axis=2)
        summed = summed * factor[:, :, None] + jnp.einsum(
            "hqk,khd->hqd",
            weights.astype(jnp.bfloat16),
            value_heads,
            preferred_element_type=jnp.float32,
        )
        return (top_score, totals, summed)

    shard_piece = lax.all_gather(key_value, "seq", axis=1, tiled=True)
    row_count = shard_piece.shape[1]
    fold_block_rows = math.gcd(row_count, 512)

    def inner_step(block_index, inner_state):
        part_block = lax.dynamic_slice_in_dim(
            shard_piece, block_index * fold_block_rows, fold_block_rows, 1
        )
        block_begin = block_index * fold_block_rows
        return lax.cond(
            block_begin <= last_row,
            lambda state_now: absorb(state_now, part_block, block_begin),
            lambda state_now: state_now,
            inner_state,
        )

    running = lax.fori_loop(0, row_count // fold_block_rows, inner_step, start_state)
    top_final, total_final, summed_final = running
    attended = (
        jnp.transpose(summed_final / total_final[:, :, None], (1, 0, 2))
        .reshape(tok_rows, HEADS * HEAD_DIM)
        .astype(jnp.bfloat16)
    )
    residual = hidden[0].astype(jnp.float32) + jnp.dot(
        attended, out_weight, preferred_element_type=jnp.float32
    )
    center = residual - jnp.mean(residual, axis=1, keepdims=True)
    spread = jnp.mean(center * center, axis=1, keepdims=True)
    normed = (center * lax.rsqrt(spread + NORM_EPSILON) * final_gain).astype(jnp.bfloat16)
    gathered_rows, gathered_targets = (
        gathered_by_axis(normed[None], DOC, (0, 1), 0),
        gathered_by_axis(targets, DOC, (0, 1), 0),
    )
    doc_count = gathered_rows.shape[0]
    row_total = doc_count * tok_rows
    flat_rows = gathered_rows.reshape(row_total, HEADS * HEAD_DIM)
    flat_targets = gathered_targets.reshape(row_total)
    vocab_share = unembed.shape[1]
    doc_index = lax.axis_index(DOC)
    offset = doc_index * vocab_share
    block_rows = math.gcd(row_total, 512)

    def shard_stats(block_index):
        begin_at = block_index * block_rows
        block = lax.dynamic_slice_in_dim(flat_rows, begin_at, block_rows, 0)
        logits = jnp.dot(block, unembed, preferred_element_type=jnp.float32)
        top_score = jnp.max(logits, axis=1)
        totals = jnp.sum(jnp.exp(logits - top_score[:, None]), axis=1)
        wanted = lax.dynamic_slice_in_dim(flat_targets, begin_at, block_rows, 0) - offset
        matches = jnp.arange(vocab_share, dtype=jnp.int32)[None, :] == wanted[:, None]
        picked = jnp.sum(jnp.where(matches, logits, 0.0), axis=1)
        return (top_score, totals, picked)

    tops, totals, picks = lax.map(shard_stats, jnp.arange(row_total // block_rows, dtype=jnp.int32))
    tops = tops.reshape(doc_count, tok_rows)
    totals = totals.reshape(doc_count, tok_rows)
    picks = picks.reshape(doc_count, tok_rows)
    top_all, total_all, pick_all = joined_all((tops, totals, picks), DOC, combine)
    is_valid = query_place[None, :] < lengths[:, None]
    token_all = jnp.where(is_valid, top_all + jnp.log(total_all) - pick_all, 0.0)
    doc_sums = over_copies(jnp.sum(token_all, axis=1), "seq")
    log_perplexity = doc_sums / lengths.astype(jnp.float32)
    token_own = lax.dynamic_slice_in_dim(token_all, doc_index, 1, 0)
    acceptance = accept(log_perplexity, keep_rank)
    return (token_own, log_perplexity, acceptance)


def solution(mesh):
    split = Mesh(mesh.devices.reshape(mesh.shape["seq"], 2, 8), ("seq", "doc_0", "doc_1"))
    placed = (
        P(DOC, "seq", None),
        P(DOC, "seq", None),
        P(DOC, "seq", None),
        P(DOC, "seq", None),
        P(DOC, "seq"),
        P(),
        P(),
        P(),
        P(),
        P(None, DOC),
    )
    return jax.shard_map(
        shards, mesh=split, in_specs=placed, out_specs=(P(DOC, "seq"), P(), P()), check_vma=False
    )
```

profile of v0, /device:TPU:1, one launch (start us, length us, event | category | flops | bytes accessed | tf_op | source)
XLA Modules:
  0.0 322.7 jit_solution(12917053944295169730)
XLA Ops:
  7.2 1.2 copy.39
  8.5 1.1 copy.41
  9.6 1.1 copy.40
  10.7 0.1 multiply_cosine_fusion
  10.9 0.8 pad_maximum_fusion
  11.8 140.8 %all-gather.8.cloned.1.call-done = bf16[2,4096,768]{1,2,0:T(8,128)(2,1)} async-done(((bf16[2,128,768]{1,2,0:T(8,128)(2,1)}), bf16[2,4096,768]{1,2,0:T(8,128)(2,1)}) %all-gather.8.cloned.1.call-update) | async-done | bytes 12582928 | tf_op jit(solution)/shard_map/all_gather | solution.py:180
  152.7 4.8 %while.33 = (s32[]{:T(128)}, f32[12,128]{1,0:T(8,128)S(1)}, f32[12,128]{1,0:T(8,128)S(1)}, f32[12,128,64]{1,2,0:T(8,128)S(1)}, s32[]{:T(128)}, /*index=5*/bf16[2...) while((s32[]{:T(128)}, f32[12,128]{1,0:T(8,128)S(1)}, ...), condition=%wide.region_5.6_spmd.clone, body=%wide.region_0.5_spmd.clone.sunk | while | flops 211816064 | bytes 15505717 | solution.py:196
  152.8 4.4 %conditional.3 = ((f32[12,128]{1,0:T(8,128)S(1)}, f32[12,128]{1,0:T(8,128)S(1)}, f32[12,128,64]{1,2,0:T(8,128)S(1)})) conditional(s32[]{:T(128)} %convert_element_type.107, (f32[12,128]{1,0:T(8,128)S(1)}, f32[12,128]{1,0:T(8,128)S(1)}, f32[12,128,64]{1,2,0:T(8,128)S(1)}) %tuple.89, (s32[]{:T(128)}, s32[]{:T(128)}, bf16[2,4096,768]{1,2,0:T(8,128)(2,1)}, ...), branch_computations={%region_1.0_spmd, %region_2.4_spmd} | conditional | flops 211816064 | bytes 15504990 | solution.py:189
  152.8 1.5 constant_dynamic-slice_fusion.1
  154.3 0.1 broadcast_compare_fusion
  154.5 0.8 fusion.2
  155.3 0.7 fusion.4
  156.0 1.1 fusion.8
  157.6 0.4 fusion.32
  158.1 0.2 multiply_reduce_fusion
  158.3 0.1 multiply_convert_fusion
  158.5 7.0 %all-gather = bf16[256,768]{1,0:T(8,128)(2,1)} all-gather(bf16[128,768]{1,0:T(8,128)(2,1)S(1)} %multiply_convert_fusion), channel_id=2, replica_groups=mesh['seq'=32,'doc_0'=2,'doc_1'=8] {'doc_0'}, dimensions={0}, use_global_device_ids=true | all-gather | bytes 589824 | tf_op jit(solution)/shard_map/all_gather | solution.py:27
  165.5 3.1 all-gather.3
  168.6 13.5 %all-gather.4 = s32[8,2,128]{2,1,0:T(2,128)S(1)} all-gather(s32[1,2,128]{2,1,0:T(2,128)S(1)} %bitcast.81), channel_id=4, replica_groups=mesh['seq'=32,'doc_0'=2,'doc_1'=8] {'doc_1'}, dimensions={0}, use_global_device_ids=true | all-gather | bytes 9216 | tf_op jit(solution)/shard_map/all_gather | solution.py:27
  182.1 59.3 %all-gather.10.cloned.1.call-done = bf16[16,1,128,768]{3,2,1,0:T(8,128)(2,1)} async-done(((bf16[2,1,128,768]{3,2,1,0:T(8,128)(2,1)}), bf16[16,1,128,768]{3,2,1,0:T(8,128)(2,1)}) %all-gather.10.cloned.1.call-update) | async-done | bytes 3145744 | tf_op jit(solution)/shard_map/all_gather | solution.py:27
  241.4 3.9 %copy.43 = bf16[2,8,1,128,768]{4,3,1,0,2:T(8,128)(2,1)} copy(bf16[2,8,1,128,768]{4,3,0,1,2:T(8,128)(2,1)} %bitcast.69) | data formatting | bytes 6291456 | tf_op jit(solution)/shard_map/transpose | solution.py:31
  245.3 25.4 %while.32 = (s32[]{:T(128)}, f32[4,512]{1,0:T(4,128)S(1)}, f32[4,512]{1,0:T(4,128)S(1)}, f32[4,512]{1,0:T(4,128)S(1)}, s32[4]{0:T(128)S(1)}, /*index=5*/bf16[204...) while((s32[]{:T(128)}, f32[4,512]{1,0:T(4,128)S(1)}, ...), condition=%wide.region_12.13_spmd, body=%wide.region_8.12_spmd.sunk | while | flops 1313733632 | bytes 10184911 | solution.py:233
  245.3 0.6 dynamic_slice.37
  246.5 3.7 %fusion.42 = (f32[512]{0:T(512)S(1)}, f32[512,1664]{1,0:T(8,128)S(1)}) fusion(bf16[768,1664]{1,0:T(8,128)(2,1)} %get-tuple-element.568, bf16[2048,768]{1,0:T(8,128)(2,1)} %get-tuple-element.567, s32[]{:T(128)S(6)} %select_n.101), kind=kOutput, calls=%fused_computation.76.clone.1 | convolution fusion | flops 1309474304 | bytes 6752260 | tf_op jit(solution)/shard_map/while/body/eval_jaxpr/dot_general | solution.py:225
  250.3 1.2 select_reduce_fusion.2
  251.6 0.6 dynamic_slice.37
  252.9 3.7 %fusion.42 = (f32[512]{0:T(512)S(1)}, f32[512,1664]{1,0:T(8,128)S(1)}) fusion(bf16[768,1664]{1,0:T(8,128)(2,1)} %get-tuple-element.568, bf16[2048,768]{1,0:T(8,128)(2,1)} %get-tuple-element.567, s32[]{:T(128)S(6)} %select_n.101), kind=kOutput, calls=%fused_computation.76.clone.1 | convolution fusion | flops 1309474304 | bytes 6752260 | tf_op jit(solution)/shard_map/while/body/eval_jaxpr/dot_general | solution.py:225
  256.5 0.1 dynamic-slice_subtract_fusion.2
  256.6 1.2 select_reduce_fusion.2
  258.0 0.6 dynamic_slice.37
  259.2 3.7 %fusion.42 = (f32[512]{0:T(512)S(1)}, f32[512,1664]{1,0:T(8,128)S(1)}) fusion(bf16[768,1664]{1,0:T(8,128)(2,1)} %get-tuple-element.568, bf16[2048,768]{1,0:T(8,128)(2,1)} %get-tuple-element.567, s32[]{:T(128)S(6)} %select_n.101), kind=kOutput, calls=%fused_computation.76.clone.1 | convolution fusion | flops 1309474304 | bytes 6752260 | tf_op jit(solution)/shard_map/while/body/eval_jaxpr/dot_general | solution.py:225
  263.0 1.2 select_reduce_fusion.2
  264.4 0.6 dynamic_slice.37
  265.6 3.7 %fusion.42 = (f32[512]{0:T(512)S(1)}, f32[512,1664]{1,0:T(8,128)S(1)}) fusion(bf16[768,1664]{1,0:T(8,128)(2,1)} %get-tuple-element.568, bf16[2048,768]{1,0:T(8,128)(2,1)} %get-tuple-element.567, s32[]{:T(128)S(6)} %select_n.101), kind=kOutput, calls=%fused_computation.76.clone.1 | convolution fusion | flops 1309474304 | bytes 6752260 | tf_op jit(solution)/shard_map/while/body/eval_jaxpr/dot_general | solution.py:225
  269.3 1.2 select_reduce_fusion.2
  270.8 0.8 broadcast_in_dim.91
  271.5 4.9 %all-to-all-start = ((f32[16,48,128]{2,1,0:T(8,128)}), f32[16,48,128]{2,1,0:T(8,128)S(1)}, u32[]{:S(2)}, u32[]{:S(2)}) async-start(f32[16,48,128]{2,1,0:T(8,128)} %broadcast_in_dim.91), calls=%async_computation | async-start | bytes 786432 | tf_op jit(solution)/shard_map/all_to_all | solution.py:40
  277.1 10.4 %all-to-all-done = f32[16,48,128]{2,1,0:T(8,128)S(1)} async-done(((f32[16,48,128]{2,1,0:T(8,128)}), f32[16,48,128]{2,1,0:T(8,128)S(1)}, u32[]{:S(2)}, u32[]{:S(2)}) %all-to-all-start) | async-done | bytes 393248 | tf_op jit(solution)/shard_map/all_to_all | solution.py:40
  287.7 0.2 fusion.28
  287.8 0.6 broadcast_in_dim.93
  288.4 11.5 %all-to-all-start.1 = ((f32[32,1,16]{2,1,0:T(1,128)}), f32[32,1,16]{2,1,0:T(1,128)S(1)}, u32[]{:S(2)}, u32[]{:S(2)}) async-start(f32[32,1,16]{2,1,0:T(1,128)} %broadcast_in_dim.93), calls=%async_computation.1 | async-start | bytes 32768 | tf_op jit(solution)/shard_map/all_to_all | solution.py:40
  300.0 0.5 constant_dynamic-slice_fusion.2
  300.5 8.9 %all-to-all-done.1 = f32[32,1,16]{2,1,0:T(1,128)S(1)} async-done(((f32[32,1,16]{2,1,0:T(1,128)}), f32[32,1,16]{2,1,0:T(1,128)S(1)}, u32[]{:S(2)}, u32[]{:S(2)}) %all-to-all-start.1) | async-done | bytes 2080 | tf_op jit(solution)/shard_map/all_to_all | solution.py:40
  309.4 0.6 fusion.27
  310.0 1.4 sort.15
  311.4 0.7 fusion.25
  313.4 0.6 multiply_reduce_fusion.1
  315.3 0.5 add_divide_fusion
  (84 shorter events, 1.6 us)
Async XLA Ops:
  7.2 150.5 %copy-start = (bf16[768,768]{1,0:T(8,128)(2,1)S(1)}, bf16[768,768]{1,0:T(8,128)(2,1)}, u32[]{:S(2)}) copy-start(bf16[768,768]{1,0:T(8,128)(2,1)} %param.23) | copy-start | bytes 3538948
  7.2 145.5 %all-gather.8.cloned.1.call-start = ((), (), s32[]{:S(2)}) async-start(), calls=%async_computation.2 | async-start | bytes 12976128 | tf_op jit(solution)/shard_map/all_gather | solution.py:180
  11.7 229.7 %all-gather.10.cloned.1.call-start = ((), (), s32[]{:S(2)}) async-start(), calls=%async_computation.3 | async-start | bytes 3538944 | tf_op jit(solution)/shard_map/all_gather | solution.py:27
  152.7 4.9 %copy-start.1 = (bf16[1,128,768]{2,1,0:T(8,128)(2,1)S(1)}, bf16[1,128,768]{2,1,0:T(8,128)(2,1)}, u32[]{:S(2)}) copy-start(bf16[1,128,768]{2,1,0:T(8,128)(2,1)} %param.16) | copy-start | bytes 589828
  152.7 5.6 %copy-start.2 = (f32[768]{0:T(1024)S(1)}, f32[768]{0:T(1024)}, u32[]{:S(2)}) copy-start(f32[768]{0:T(1024)} %param.24) | copy-start | bytes 9220
  157.6 7.9 %copy-start.5 = (s32[1,128]{1,0:T(1,128)S(1)}, s32[1,128]{1,0:T(1,128)}, u32[]{:S(2)}) copy-start(s32[1,128]{1,0:T(1,128)} %param.20) | copy-start | bytes 1540
  270.7 16.9 %copy-start.3 = (s32[16]{0:T(128)S(1)}, s32[16]{0:T(128)}, u32[]{:S(2)}) copy-start(s32[16]{0:T(128)} %param.21) | copy-start | bytes 196
  271.5 15.9 %all-to-all-start = ((f32[16,48,128]{2,1,0:T(8,128)}), f32[16,48,128]{2,1,0:T(8,128)S(1)}, u32[]{:S(2)}, u32[]{:S(2)}) async-start(f32[16,48,128]{2,1,0:T(8,128)} %broadcast_in_dim.91), calls=%async_computation | async-start | bytes 786432 | tf_op jit(solution)/shard_map/all_to_all | solution.py:40
  288.4 20.9 %all-to-all-start.1 = ((f32[32,1,16]{2,1,0:T(1,128)}), f32[32,1,16]{2,1,0:T(1,128)S(1)}, u32[]{:S(2)}, u32[]{:S(2)}) async-start(f32[32,1,16]{2,1,0:T(1,128)} %broadcast_in_dim.93), calls=%async_computation.1 | async-start | bytes 32768 | tf_op jit(solution)/shard_map/all_to_all | solution.py:40
  310.0 5.8 %copy-start.4 = (f32[16]{0:T(128)}, f32[16]{0:T(128)S(1)}, u32[]{:S(2)}) copy-start(f32[16]{0:T(128)S(1)} %get-tuple-element.352) | copy-start | bytes 196
Sparse Core Ops, SparseCore 0:
  11.9 140.7 all-gather.7
  165.6 75.8 all-gather.9
where the time goes:
time: 323 us
  waiting for transfers between devices  219 us (68%)
  blocking collectives  23.5 us (7%)
  between operations  17.7 us (5%)
  matrix products  17 us (5%)
  starting transfers between devices  16.5 us (5%)
  local copies, waits for them, and re-layouts  13.8 us (4%)
  other arithmetic  11.6 us (4%)
    all_gather x1, waiting for transfers between devices, shards(): shard_piece = lax.all_gather(key_value, 'seq', axis=1, tiled=True)  141 us
    all_gather x1, waiting for transfers between devices, all_blocks(): blocks = lax.all_gather(blocks, axes[k], axis=0, tiled=True)  59.3 us
    all_gather x3, blocking collectives, all_blocks(): blocks = lax.all_gather(blocks, axes[k], axis=0, tiled=True)  23.5 us
    all_to_all x2, waiting for transfers between devices, from_everyone(): return lax.all_to_all(copies, axis, split_axis=0, concat_axis=0, tiled=True)  19.3 us
    all_to_all x2, starting transfers between devices, from_everyone(): return lax.all_to_all(copies, axis, split_axis=0, concat_axis=0, tiled=True)  16.4 us
    dot_general x4, matrix products, shard_stats(): logits = jnp.dot(block, unembed, preferred_element_type=jnp.float32)  14.6 us
  transfers between devices with their start and end apart: 4, of which 4 were waited for; matrix products, arithmetic and copies ran while one was open for 0% of the time, Pallas kernels for 0%

commit v1 on v0

--- a/solution.py
+++ b/solution.py
@@ -24,7 +24,14 @@
 def all_blocks(array, axes, turns):
     blocks = array[None]
     for k in turns:
-        blocks = lax.all_gather(blocks, axes[k], axis=0, tiled=True)
+        incoming_x = axes[k]
+        base_arr = lax.all_to_all(
+            jnp.stack([blocks for _ in range(lax.psum(1, axis_name=incoming_x))], axis=0),
+            axis_name=incoming_x,
+            concat_axis=0,
+            split_axis=0,
+        )
+        blocks = jnp.concatenate(base_arr, axis=0)
     held = [lax.axis_size(axes[k]) for k in reversed(turns)]
     blocks = blocks.reshape(*held, *array.shape)
     turned = sorted(range(len(turns)), key=lambda place: turns[len(turns) - 1 - place])

time: 323 us -> 357 us (1.11)
  starting transfers between devices: 16.5 us -> 61.7 us
  blocking collectives: 23.5 us -> 8.81 us
    all_to_all x0 -> x3, waiting for transfers between devices: none -> 77.3 us  [all_blocks(): lax.all_to_all(jnp.stack([blocks for _ in range(lax.psum(1, axis_name=inc...]
    all_gather x1 -> x0, waiting for transfers between devices: 59.3 us -> none  [all_blocks(): blocks = lax.all_gather(blocks, axes[k], axis=0, tiled=True)]
    all_to_all x2, starting transfers between devices: 16.4 us -> 41 us  [from_everyone(): return lax.all_to_all(copies, axis, split_axis=0, concat_axis=0, tiled=True)]
    all_gather x3 -> x0, blocking collectives: 23.5 us -> none  [all_blocks(): blocks = lax.all_gather(blocks, axes[k], axis=0, tiled=True)]
    all_to_all x0 -> x3, starting transfers between devices: none -> 20.7 us  [all_blocks(): lax.all_to_all(jnp.stack([blocks for _ in range(lax.psum(1, axis_name=inc...]
    all_gather x1, waiting for transfers between devices: 141 us -> 123 us  [shards(): shard_piece = lax.all_gather(key_value, 'seq', axis=1, tiled=True)]
    all_to_all x0 -> x1, blocking collectives: none -> 8.81 us  [all_blocks(): lax.all_to_all(jnp.stack([blocks for _ in range(lax.psum(1, axis_name=inc...]
    all_to_all x0 -> x2, local copies, waits for them, and re-layouts: none -> 3.87 us  [all_blocks(): lax.all_to_all(jnp.stack([blocks for _ in range(lax.psum(1, axis_name=inc...]
  transfers between devices with their start and end apart: 4 -> 6, of which waited for: 4 -> 5; matrix products, arithmetic and copies ran while one was open for 0% -> 2% of each run, Pallas kernels for 0% -> 0%
where the time goes in v1:
time: 357 us
  waiting for transfers between devices  220 us (62%)
  starting transfers between devices  61.7 us (17%)
  between operations  17.7 us (5%)
  matrix products  17 us (5%)
  local copies, waits for them, and re-layouts  16.4 us (5%)
  other arithmetic  12.2 us (3%)
  blocking collectives  8.81 us (2%)
    all_gather x1, waiting for transfers between devices, shards(): shard_piece = lax.all_gather(key_value, 'seq', axis=1, tiled=True)  123 us
    all_to_all x3, waiting for transfers between devices, all_blocks(): lax.all_to_all(jnp.stack([blocks for _ in range(lax.psum(1, axis_name=inc...  77.3 us
    all_to_all x2, starting transfers between devices, from_everyone(): return lax.all_to_all(copies, axis, split_axis=0, concat_axis=0, tiled=True)  41 us
    all_to_all x3, starting transfers between devices, all_blocks(): lax.all_to_all(jnp.stack([blocks for _ in range(lax.psum(1, axis_name=inc...  20.7 us
    all_to_all x2, waiting for transfers between devices, from_everyone(): return lax.all_to_all(copies, axis, split_axis=0, concat_axis=0, tiled=True)  19.3 us
    dot_general x4, matrix products, shard_stats(): logits = jnp.dot(block, unembed, preferred_element_type=jnp.float32)  14.6 us
    all_to_all x1, blocking collectives, all_blocks(): lax.all_to_all(jnp.stack([blocks for _ in range(lax.psum(1, axis_name=inc...  8.81 us
  transfers between devices with their start and end apart: 6, of which 5 were waited for; matrix products, arithmetic and copies ran while one was open for 2% of the time, Pallas kernels for 0%

profile of v1, /device:TPU:1, one launch (start us, length us, event | category | flops | bytes accessed | tf_op | source)
XLA Modules:
  0.0 356.6 jit_solution(2756570905811912718)
XLA Ops:
  7.3 1.2 copy.39
  8.5 1.1 copy.41
  9.6 1.1 copy.40
  10.9 0.8 pad_maximum_fusion
  11.8 0.6 pad_add_fusion
  12.3 3.3 all-to-all-start.2
  15.7 3.0 all-to-all-done.2
  18.7 0.6 stack.20
  19.3 10.3 %all-to-all-start.3 = ((s32[8,2,1,128]{3,1,2,0:T(2,128)}), s32[8,2,1,128]{3,1,2,0:T(2,128)S(1)}, u32[]{:S(2)}, u32[]{:S(2)}) async-start(s32[8,2,1,128]{3,1,2,0:T(2,128)} %stack.20), calls=%async_computation.3 | async-start | bytes 16384 | tf_op jit(solution)/shard_map/all_to_all | solution.py:28
  29.6 123.1 %all-gather.2.cloned.1.call-done = bf16[2,4096,768]{1,2,0:T(8,128)(2,1)} async-done(((bf16[2,128,768]{1,2,0:T(8,128)(2,1)}), bf16[2,4096,768]{1,2,0:T(8,128)(2,1)}) %all-gather.2.cloned.1.call-update) | async-done | bytes 12582928 | tf_op jit(solution)/shard_map/all_gather | solution.py:187
  152.7 4.8 %while.33 = (s32[]{:T(128)}, f32[12,128]{1,0:T(8,128)S(1)}, f32[12,128]{1,0:T(8,128)S(1)}, f32[12,128,64]{1,2,0:T(8,128)S(1)}, s32[]{:T(128)}, /*index=5*/bf16[2...) while((s32[]{:T(128)}, f32[12,128]{1,0:T(8,128)S(1)}, ...), condition=%wide.region_5.6_spmd.clone, body=%wide.region_0.5_spmd.clone.sunk | while | flops 211816064 | bytes 15505717 | solution.py:203
  152.8 4.4 %conditional.3 = ((f32[12,128]{1,0:T(8,128)S(1)}, f32[12,128]{1,0:T(8,128)S(1)}, f32[12,128,64]{1,2,0:T(8,128)S(1)})) conditional(s32[]{:T(128)} %convert_element_type.109, (f32[12,128]{1,0:T(8,128)S(1)}, f32[12,128]{1,0:T(8,128)S(1)}, f32[12,128,64]{1,2,0:T(8,128)S(1)}) %tuple.89, (s32[]{:T(128)}, s32[]{:T(128)}, bf16[2,4096,768]{1,2,0:T(8,128)(2,1)}, ...), branch_computations={%region_1.0_spmd, %region_2.4_spmd} | conditional | flops 211816064 | bytes 15504990 | solution.py:196
  152.8 1.5 constant_dynamic-slice_fusion.1
  154.5 0.8 fusion.2
  155.3 0.7 fusion.4
  156.0 1.1 fusion.8
  157.6 0.4 fusion.33
  158.1 0.2 multiply_reduce_fusion
  158.5 8.8 %all_to_all.31 = bf16[2,1,1,128,768]{4,3,2,1,0:T(8,128)(2,1)S(1)} all-to-all(bf16[2,1,1,128,768]{4,3,2,1,0:T(8,128)(2,1)S(1)} %pad_maximum_fusion.1), channel_id=1, replica_groups=mesh['seq'=32,'doc_0'=2,'doc_1'=8] {'doc_0'}, dimensions={0} | all-to-all | bytes 786432 | tf_op jit(solution)/shard_map/all_to_all | solution.py:28
  167.3 2.0 stack.18
  169.3 7.1 %all-to-all-start.1 = ((bf16[8,2,1,128,768]{4,3,1,2,0:T(8,128)(2,1)}), bf16[8,2,1,128,768]{4,3,1,2,0:T(8,128)(2,1)}, u32[]{:S(2)}, u32[]{:S(2)}) async-start(bf16[8,2,1,128,768]{4,3,1,2,0:T(8,128)(2,1)} %stack.18), calls=%async_computation.1 | async-start | bytes 6291456 | tf_op jit(solution)/shard_map/all_to_all | solution.py:28
  176.4 74.3 %all-to-all-done.1 = bf16[8,2,1,128,768]{4,3,1,2,0:T(8,128)(2,1)} async-done(((bf16[8,2,1,128,768]{4,3,1,2,0:T(8,128)(2,1)}), bf16[8,2,1,128,768]{4,3,1,2,0:T(8,128)(2,1)}, u32[]{:S(2)}, u32[]{:S(2)}) %all-to-all-start.1) | async-done | bytes 3145760 | tf_op jit(solution)/shard_map/all_to_all | solution.py:28
  250.7 3.9 %copy.42 = bf16[8,2,1,128,768]{4,3,0,1,2:T(8,128)(2,1)} copy(bf16[8,2,1,128,768]{4,3,1,2,0:T(8,128)(2,1)} %all-to-all-done.1) | data formatting | bytes 6291456 | tf_op jit(solution)/shard_map/all_to_all | solution.py:28
  254.6 25.4 %while.32 = (s32[]{:T(128)}, f32[4,512]{1,0:T(4,128)S(1)}, f32[4,512]{1,0:T(4,128)S(1)}, f32[4,512]{1,0:T(4,128)S(1)}, s32[4]{0:T(128)S(1)}, /*index=5*/bf16[204...) while((s32[]{:T(128)}, f32[4,512]{1,0:T(4,128)S(1)}, ...), condition=%wide.region_12.13_spmd, body=%wide.region_8.12_spmd.sunk | while | flops 1313733632 | bytes 10184911 | solution.py:240
  254.6 0.6 dynamic_slice.37
  255.8 3.7 %fusion.43 = (f32[512]{0:T(512)S(1)}, f32[512,1664]{1,0:T(8,128)S(1)}) fusion(bf16[768,1664]{1,0:T(8,128)(2,1)} %get-tuple-element.568, bf16[2048,768]{1,0:T(8,128)(2,1)} %get-tuple-element.567, s32[]{:T(128)S(6)} %select_n.101), kind=kOutput, calls=%fused_computation.79.clone.1 | convolution fusion | flops 1309474304 | bytes 6752260 | tf_op jit(solution)/shard_map/while/body/eval_jaxpr/dot_general | solution.py:232
  259.6 1.2 select_reduce_fusion.2
  260.9 0.6 dynamic_slice.37
  262.2 3.7 %fusion.43 = (f32[512]{0:T(512)S(1)}, f32[512,1664]{1,0:T(8,128)S(1)}) fusion(bf16[768,1664]{1,0:T(8,128)(2,1)} %get-tuple-element.568, bf16[2048,768]{1,0:T(8,128)(2,1)} %get-tuple-element.567, s32[]{:T(128)S(6)} %select_n.101), kind=kOutput, calls=%fused_computation.79.clone.1 | convolution fusion | flops 1309474304 | bytes 6752260 | tf_op jit(solution)/shard_map/while/body/eval_jaxpr/dot_general | solution.py:232
  265.9 1.2 select_reduce_fusion.2
  267.3 0.6 dynamic_slice.37
  268.5 3.7 %fusion.43 = (f32[512]{0:T(512)S(1)}, f32[512,1664]{1,0:T(8,128)S(1)}) fusion(bf16[768,1664]{1,0:T(8,128)(2,1)} %get-tuple-element.568, bf16[2048,768]{1,0:T(8,128)(2,1)} %get-tuple-element.567, s32[]{:T(128)S(6)} %select_n.101), kind=kOutput, calls=%fused_computation.79.clone.1 | convolution fusion | flops 1309474304 | bytes 6752260 | tf_op jit(solution)/shard_map/while/body/eval_jaxpr/dot_general | solution.py:232
  272.3 1.2 select_reduce_fusion.2
  273.7 0.6 dynamic_slice.37
  274.9 3.7 %fusion.43 = (f32[512]{0:T(512)S(1)}, f32[512,1664]{1,0:T(8,128)S(1)}) fusion(bf16[768,1664]{1,0:T(8,128)(2,1)} %get-tuple-element.568, bf16[2048,768]{1,0:T(8,128)(2,1)} %get-tuple-element.567, s32[]{:T(128)S(6)} %select_n.101), kind=kOutput, calls=%fused_computation.79.clone.1 | convolution fusion | flops 1309474304 | bytes 6752260 | tf_op jit(solution)/shard_map/while/body/eval_jaxpr/dot_general | solution.py:232
  278.6 1.2 select_reduce_fusion.2
  280.1 0.8 broadcast_in_dim.87
  280.8 3.6 all-to-all-start.4
  285.1 10.5 %all-to-all-done.4 = f32[16,48,128]{2,1,0:T(8,128)S(1)} async-done(((f32[16,48,128]{2,1,0:T(8,128)}), f32[16,48,128]{2,1,0:T(8,128)S(1)}, u32[]{:S(2)}, u32[]{:S(2)}) %all-to-all-start.4) | async-done | bytes 393248 | tf_op jit(solution)/shard_map/all_to_all | solution.py:47
  295.9 0.6 broadcast_in_dim.89
  296.5 37.4 %all-to-all-start.5 = ((f32[32,1,16]{2,1,0:T(1,128)}), f32[32,1,16]{2,1,0:T(1,128)S(1)}, u32[]{:S(2)}, u32[]{:S(2)}) async-start(f32[32,1,16]{2,1,0:T(1,128)} %broadcast_in_dim.89), calls=%async_computation.5 | async-start | bytes 32768 | tf_op jit(solution)/shard_map/all_to_all | solution.py:47
  333.9 0.5 constant_dynamic-slice_fusion.2
  334.5 8.9 %all-to-all-done.5 = f32[32,1,16]{2,1,0:T(1,128)S(1)} async-done(((f32[32,1,16]{2,1,0:T(1,128)}), f32[32,1,16]{2,1,0:T(1,128)S(1)}, u32[]{:S(2)}, u32[]{:S(2)}) %all-to-all-start.5) | async-done | bytes 2080 | tf_op jit(solution)/shard_map/all_to_all | solution.py:47
  343.4 0.6 fusion.28
  344.0 1.4 sort.15
  345.3 0.7 fusion.26
  347.4 0.6 multiply_reduce_fusion.1
  349.2 0.5 add_divide_fusion
  (89 shorter events, 2.2 us)
Async XLA Ops:
  7.2 150.5 %copy-start = (bf16[768,768]{1,0:T(8,128)(2,1)S(1)}, bf16[768,768]{1,0:T(8,128)(2,1)}, u32[]{:S(2)}) copy-start(bf16[768,768]{1,0:T(8,128)(2,1)} %param.23) | copy-start | bytes 3538948
  7.2 4.6 %copy-start.5 = (s32[1,128]{1,0:T(1,128)S(1)}, s32[1,128]{1,0:T(1,128)}, u32[]{:S(2)}) copy-start(s32[1,128]{1,0:T(1,128)} %param.20) | copy-start | bytes 1540
  7.2 145.5 %all-gather.2.cloned.1.call-start = ((), (), s32[]{:S(2)}) async-start(), calls=%async_computation.6 | async-start | bytes 12976128 | tf_op jit(solution)/shard_map/all_gather | solution.py:187
  12.3 6.4 %all-to-all-start.2 = ((s32[2,1,1,128]{3,2,1,0:T(1,128)}), s32[2,1,1,128]{3,2,1,0:T(1,128)S(1)}, u32[]{:S(2)}, u32[]{:S(2)}) async-start(s32[2,1,1,128]{3,2,1,0:T(1,128)} %pad_add_fusion), calls=%async_computation.2 | async-start | bytes 2048 | tf_op jit(solution)/shard_map/all_to_all | solution.py:28
  19.3 139.2 %all-to-all-start.3 = ((s32[8,2,1,128]{3,1,2,0:T(2,128)}), s32[8,2,1,128]{3,1,2,0:T(2,128)S(1)}, u32[]{:S(2)}, u32[]{:S(2)}) async-start(s32[8,2,1,128]{3,1,2,0:T(2,128)} %stack.20), calls=%async_computation.3 | async-start | bytes 16384 | tf_op jit(solution)/shard_map/all_to_all | solution.py:28
  152.7 4.9 %copy-start.1 = (bf16[1,128,768]{2,1,0:T(8,128)(2,1)S(1)}, bf16[1,128,768]{2,1,0:T(8,128)(2,1)}, u32[]{:S(2)}) copy-start(bf16[1,128,768]{2,1,0:T(8,128)(2,1)} %param.16) | copy-start | bytes 589828
  152.7 5.6 %copy-start.2 = (f32[768]{0:T(1024)S(1)}, f32[768]{0:T(1024)}, u32[]{:S(2)}) copy-start(f32[768]{0:T(1024)} %param.24) | copy-start | bytes 9220
  169.3 81.4 %all-to-all-start.1 = ((bf16[8,2,1,128,768]{4,3,1,2,0:T(8,128)(2,1)}), bf16[8,2,1,128,768]{4,3,1,2,0:T(8,128)(2,1)}, u32[]{:S(2)}, u32[]{:S(2)}) async-start(bf16[8,2,1,128,768]{4,3,1,2,0:T(8,128)(2,1)} %stack.18), calls=%async_computation.1 | async-start | bytes 6291456 | tf_op jit(solution)/shard_map/all_to_all | solution.py:28
  280.0 15.7 %copy-start.3 = (s32[16]{0:T(128)S(1)}, s32[16]{0:T(128)}, u32[]{:S(2)}) copy-start(s32[16]{0:T(128)} %param.21) | copy-start | bytes 196
  280.8 14.7 %all-to-all-start.4 = ((f32[16,48,128]{2,1,0:T(8,128)}), f32[16,48,128]{2,1,0:T(8,128)S(1)}, u32[]{:S(2)}, u32[]{:S(2)}) async-start(f32[16,48,128]{2,1,0:T(8,128)} %broadcast_in_dim.87), calls=%async_computation.4 | async-start | bytes 786432 | tf_op jit(solution)/shard_map/all_to_all | solution.py:47
  296.5 46.8 %all-to-all-start.5 = ((f32[32,1,16]{2,1,0:T(1,128)}), f32[32,1,16]{2,1,0:T(1,128)S(1)}, u32[]{:S(2)}, u32[]{:S(2)}) async-start(f32[32,1,16]{2,1,0:T(1,128)} %broadcast_in_dim.89), calls=%async_computation.5 | async-start | bytes 32768 | tf_op jit(solution)/shard_map/all_to_all | solution.py:47
  344.0 5.8 %copy-start.4 = (f32[16]{0:T(128)}, f32[16]{0:T(128)S(1)}, u32[]{:S(2)}) copy-start(f32[16]{0:T(128)S(1)} %get-tuple-element.352) | copy-start | bytes 196
Sparse Core Ops, SparseCore 0:
  11.9 140.7 all-gather.1
